TPU v7x, 32 devices: a whole 2x2x4 slice. The times are simulated.
32 devices in a mesh: rep: 4 (over z), tok: 4 (over x, core), voc: 2 (over y).
Axes of the slice: x: 2, y: 2, z: 4, core: 2. Of those that a mesh axis runs over, the one named last changes fastest.
Arguments:
- hidden: bfloat16 [4, 64, 4096], P('rep', ('tok', 'voc')), may hold values from -500 to 500
- targets: int32 [4, 64], P('rep', ('tok', 'voc')), may hold values from 0 to 8191
- unembed: bfloat16 [4, 8192, 4096], P('rep', ('tok', 'voc')), may hold values from -1 to 1
- outer_weight: float32 [1024, 4096], P(('tok', 'voc'), 'rep'), may hold values from -0.9 to 0.9
- momentum: float32 [1024, 4096], P(('tok', 'voc'), 'rep'), may hold values from -0.18 to 0.18
Outputs:
- token_loss: float32 [4, 64], P('rep', ('tok', 'voc'))
- hidden_grad: float32 [4, 64, 4096], P('rep', ('tok', 'voc'))
- new_outer: float32 [1024, 4096], P(('tok', 'voc'), 'rep')
- new_momentum: float32 [1024, 4096], P(('tok', 'voc'), 'rep')
- next_inner: bfloat16 [1024, 4096], P(('tok', 'voc'))
All inputs are finite; a program needn't handle non-finite values.
Results may differ from a plain program's by a relative error of at most 0.0085.
Values may be sent and summed in bfloat16 or wider, within the bound.
A program may use at most 64 MiB of HBM per device.

v0:
```python
import jax
import jax.numpy as jnp
from jax import lax
from jax.sharding import PartitionSpec as P

inner_rate = 0.5
outer_rate = 0.7
momentum_coef = 0.9


def nesterov(outer_part, momentum_part, mean_final):
    pseudo_grad = outer_part - mean_final
    moved_momentum = momentum_coef * momentum_part + pseudo_grad
    moved_outer = outer_part - outer_rate * (pseudo_grad + momentum_coef * moved_momentum)
    return (moved_outer, moved_momentum)


def per_device(hidden, targets, unembed, outer_weight, momentum):
    weights = unembed[0]
    vocab_rows, model_width = weights.shape
    tok_rows = hidden.shape[1]
    slab_rows = outer_weight.shape[0]
    logit_scale = model_width ** (-0.5)
    group_index = lax.axis_index("tok") * lax.axis_size("voc") + lax.axis_index("voc")
    every_hidden, every_target = (
        lax.all_gather(hidden[0], ("tok", "voc"), axis=0, tiled=True),
        lax.all_gather(targets[0], ("tok", "voc"), axis=0, tiled=True),
    )
    logits = (
        jnp.einsum("td,vd->tv", every_hidden, weights, preferred_element_type=jnp.float32)
        * logit_scale
    )
    columns = group_index * vocab_rows + lax.broadcasted_iota(jnp.int32, (1, vocab_rows), 1)
    onehot = every_target[:, None] == columns
    target_part = jnp.sum(jnp.where(onehot, logits, 0.0), axis=1)
    row_top = lax.pmax(jnp.max(logits, axis=1), ("tok", "voc"))
    local_total = jnp.sum(jnp.exp(logits - row_top[:, None]), axis=1)
    row_total, target_logit = lax.psum((local_total, target_part), ("tok", "voc"))
    log_total = row_top + jnp.log(row_total)
    every_loss = log_total - target_logit
    token_loss = lax.dynamic_slice_in_dim(every_loss, group_index * tok_rows, tok_rows)[None]
    errors = (jnp.exp(logits - log_total[:, None]) - onehot.astype(jnp.float32)).astype(
        jnp.bfloat16
    )
    token_grad = lax.psum_scatter(
        jnp.dot(errors, weights, preferred_element_type=jnp.float32) * logit_scale,
        ("tok", "voc"),
        scatter_dimension=0,
        tiled=True,
    )
    slab_errors = errors[:, :slab_rows]
    slab_grad = (
        jnp.einsum("tv,td->vd", slab_errors, every_hidden, preferred_element_type=jnp.float32)
        * logit_scale
    )
    final_slab = weights[:slab_rows].astype(jnp.float32) - inner_rate * slab_grad
    replicas = lax.axis_size("rep")
    mean_final = lax.psum_scatter(final_slab, "rep", scatter_dimension=1, tiled=True) / replicas
    new_outer, new_momentum = nesterov(outer_weight, momentum, mean_final)
    next_inner = lax.all_gather(new_outer.astype(jnp.bfloat16), "rep", axis=1, tiled=True)
    return (token_loss, token_grad[None], new_outer, new_momentum, next_inner)


def solution(mesh):
    return jax.shard_map(
        per_device,
        mesh=mesh,
        in_specs=(
            P("rep", ("tok", "voc"), None),
            P("rep", ("tok", "voc")),
            P("rep", ("tok", "voc"), None),
            P(("tok", "voc"), "rep"),
            P(("tok", "voc"), "rep"),
        ),
        out_specs=(
            P("rep", ("tok", "voc")),
            P("rep", ("tok", "voc"), None),
            P(("tok", "voc"), "rep"),
            P(("tok", "voc"), "rep"),
            P(("tok", "voc"), None),
        ),
        check_vma=False,
    )
```

profile of v0, /device:TPU:0, one launch (start us, length us, event | category | flops | bytes accessed | tf_op | source)
XLA Modules:
  0.0 170.1 jit_solution(13773331553616933622)
XLA Ops:
  8.0 0.0 copy-start.1
  8.0 0.0 reduce-scatter.5.cloned.1.call-start
  8.1 1.3 dynamic-slice
  10.1 0.8 bitcast_dynamic-update-slice_fusion
  10.8 8.8 %all-reduce = s32[64]{0:T(128)S(1)} all-reduce(s32[64]{0:T(128)S(1)} %bitcast_dynamic-update-slice_fusion), channel_id=3, replica_groups=mesh['rep'=4,'tok'=4,'voc'=2] {'tok','voc'}, use_global_device_ids=true, to_apply=%add | all-reduce | flops 64 | bytes 512
  19.6 17.2 %all-gather = bf16[1,64,4096]{2,1,0:T(8,128)(2,1)S(1)} all-gather(bf16[1,8,4096]{2,1,0:T(8,128)(2,1)} %param.5), channel_id=2, replica_groups=mesh['rep'=4,'tok'=4,'voc'=2] {'tok','voc'}, dimensions={1}, use_global_device_ids=true | all-gather | bytes 589824 | tf_op jit(solution)/shard_map/all_gather | solution.py:26
  36.9 6.1 %fusion.19 = (f32[64]{0:T(128)S(1)}, f32[64,1024]{1,0:T(8,128)S(1)}) fusion(bf16[1,1024,4096]{2,1,0:T(8,128)(2,1)} %param.7, bf16[1,64,4096]{2,1,0:T(8,128)(2,1)S(1)} %all-gather), kind=kOutput, calls=%fused_computation.26 | convolution fusion | flops 537001920 | bytes 9175296 | tf_op jit(solution)/shard_map/td,vd->tv/dot_general | solution.py:30
  43.0 13.6 %pmax.7 = f32[64]{0:T(128)S(1)} all-reduce(f32[64]{0:T(128)S(1)} %get-tuple-element.14), channel_id=1, replica_groups=mesh['rep'=4,'tok'=4,'voc'=2] {'tok','voc'}, use_global_device_ids=true, to_apply=%region_1.2 | all-reduce | flops 64 | bytes 512 | tf_op jit(solution)/shard_map/pmax | solution.py:36
  56.6 0.2 fusion.13
  56.8 12.4 %all-reduce.1 = (f32[64]{0:T(128)S(1)}, f32[64]{0:T(128)S(1)}) all-reduce(f32[64]{0:T(128)S(1)} %get-tuple-element.6, f32[64]{0:T(128)S(1)} %get-tuple-element.5), channel_id=1, replica_groups=mesh['rep'=4,'tok'=4,'voc'=2] {'tok','voc'}, use_global_device_ids=true, to_apply=%region_3.4 | all-reduce | flops 128 | bytes 1024 | tf_op jit(solution)/shard_map/psum | solution.py:38
  69.3 0.1 fusion.15
  69.4 3.0 %fusion.4 = f32[128,4096]{1,0:T(8,128)} fusion(bf16[1,1024,4096]{2,1,0:T(8,128)(2,1)} %param.7, bf16[1,64,4096]{2,1,0:T(8,128)(2,1)S(1)} %all-gather, bf16[64,1024]{1,0:T(8,128)(2,1)S(1)} %fusion.15), kind=kOutput, calls=%fused_computation.5 | convolution fusion | flops 68681728 | bytes 3686400 | tf_op jit(solution)/shard_map/tv,td->vd/dot_general | solution.py:53
  72.4 0.0 reduce-scatter.5.cloned.1.call-update
  72.5 0.0 all-gather.4.cloned.1.call-start
  72.5 44.3 %reduce-scatter.5.cloned.1.call-done = f32[128,1024]{1,0:T(8,128)} async-done(((f32[128,4096]{1,0:T(8,128)}), f32[128,1024]{1,0:T(8,128)}) %reduce-scatter.5.cloned.1.call-update) | async-done | bytes 524304 | tf_op jit(solution)/shard_map/reduce_scatter | solution.py:58
  116.8 2.3 %fusion.17 = (bf16[128,1024]{1,0:T(8,128)(2,1)}, f32[128,1024]{1,0:T(8,128)}, f32[128,1024]{1,0:T(8,128)}) fusion(f32[128,1024]{1,0:T(8,128)S(1)} %copy-done, f32[128,1024]{1,0:T(8,128)} %reduce-scatter.5.cloned.1.call-done, f32[128,1024]{1,0:T(8,128)S(1)} %copy-done.1), kind=kLoop, calls=%fused_computation.24 | loop fusion | flops 1179648 | bytes 2883584 | tf_op jit(solution)/shard_map/convert_element_type | solution.py:60
  119.1 0.0 all-gather.4.cloned.1.call-update
  119.2 0.0 reduce-scatter.3.cloned.1.call-start
  119.2 5.9 %fusion.5 = f32[64,4096]{1,0:T(8,128)} fusion(bf16[64,1024]{1,0:T(8,128)(2,1)S(1)} %fusion.15, bf16[1,1024,4096]{2,1,0:T(8,128)(2,1)} %param.7), kind=kOutput, calls=%fused_computation.6 | convolution fusion | flops 537133056 | bytes 9568256 | tf_op jit(solution)/shard_map/dot_general | solution.py:46
  125.2 0.0 reduce-scatter.3.cloned.1.call-update
  125.2 0.6 dynamic-slice_bitcast_fusion
  125.8 20.8 %all-gather.4.cloned.1.call-done = bf16[128,4096]{1,0:T(8,128)(2,1)} async-done(((bf16[128,1024]{1,0:T(8,128)(2,1)}), bf16[128,4096]{1,0:T(8,128)(2,1)}) %all-gather.4.cloned.1.call-update) | async-done | bytes 1048592 | tf_op jit(solution)/shard_map/all_gather | solution.py:60
  146.5 13.9 %reduce-scatter.3.cloned.1.call-done = f32[8,4096]{1,0:T(8,128)} async-done(((f32[64,4096]{1,0:T(8,128)}), f32[8,4096]{1,0:T(8,128)}) %reduce-scatter.3.cloned.1.call-update) | async-done | bytes 131088 | tf_op jit(solution)/shard_map/reduce_scatter | solution.py:45
  160.4 2.3 %copy.12 = bf16[128,4096]{1,0:T(8,128)(2,1)} copy(bf16[128,4096]{1,0:T(8,128)(2,1)} %all-gather.4.cloned.1.call-done) | data formatting | bytes 2097152
  (6 shorter events, 0.0 us)
Async XLA Ops:
  8.0 108.8 %copy-start.1 = (f32[128,1024]{1,0:T(8,128)S(1)}, f32[128,1024]{1,0:T(8,128)}, u32[]{:S(2)}) copy-start(f32[128,1024]{1,0:T(8,128)} %param.9) | copy-start | bytes 1572868
  8.0 108.8 %copy-start = (f32[128,1024]{1,0:T(8,128)S(1)}, f32[128,1024]{1,0:T(8,128)}, u32[]{:S(2)}) copy-start(f32[128,1024]{1,0:T(8,128)} %param.8) | copy-start | bytes 1572868
  8.0 108.8 %reduce-scatter.5.cloned.1.call-start = ((), (), s32[]{:S(2)}) async-start(), calls=%async_computation.3 | async-start | bytes 2621440 | tf_op jit(solution)/shard_map/reduce_scatter | solution.py:58
  72.5 74.1 %all-gather.4.cloned.1.call-start = ((), (), s32[]{:S(2)}) async-start(), calls=%async_computation.4 | async-start | bytes 1310720 | tf_op jit(solution)/shard_map/all_gather | solution.py:60
  119.2 41.2 %reduce-scatter.3.cloned.1.call-start = ((), (), s32[]{:S(2)}) async-start(), calls=%async_computation.2 | async-start | bytes 1179648 | tf_op jit(solution)/shard_map/reduce_scatter | solution.py:45
Sparse Core Ops, SparseCore 0:
  72.6 44.2 reduce-scatter.4
  119.3 27.2 all-gather.3
Sparse Core Ops, SparseCore 1:
  125.3 35.1 reduce-scatter.2
where the time goes:
time: 171 us; the launch traced here: 170 us
  waiting for transfers between devices  79 us (46%)
  blocking collectives  52.1 us (30%)
  between operations  16.2 us (9%)
  matrix products  15.1 us (9%)
  local copies, waits for them, and re-layouts  4.95 us (3%)
  other arithmetic  2.67 us (2%)
    reduce_scatter x1, waiting for transfers between devices, per_device(): lax.psum_scatter(final_slab, 'rep', scatter_dimension=1, tiled=True)  44.3 us
    all_gather x1, waiting for transfers between devices, per_device(): lax.all_gather(new_outer.astype(jnp.bfloat16), 'rep', axis=1, tiled=True)  20.8 us
    all_gather x1, blocking collectives, per_device(): lax.all_gather(hidden[0], ('tok', 'voc'), axis=0, tiled=True)  17.2 us
    reduce_scatter x1, waiting for transfers between devices, per_device(): lax.psum_scatter(jnp.dot(errors, weights, preferred_element_type=jnp.floa...  13.9 us
    pmax x1, blocking collectives, per_device(): row_top = lax.pmax(jnp.max(logits, axis=1), ('tok', 'voc'))  13.6 us
    psum x1, blocking collectives, per_device(): lax.psum((local_total, target_part), ('tok', 'voc'))  12.4 us
    unnamed x1, blocking collectives  8.83 us
    dot_general x1, matrix products, per_device(): jnp.einsum('td,vd->tv', every_hidden, weights, preferred_element_type=jnp...  6.15 us
  transfers between devices with their start and end apart: 3, of which 3 were waited for; matrix products, arithmetic and copies ran while one was open for 4% of the time, Pallas kernels for 0%

commit v1 on v0

v1 whole, which is shorter than its diff:
```python
import functools

import jax
import jax.numpy as jnp
from jax import lax
from jax.experimental import pallas as pl
from jax.experimental.pallas import tpu as pltpu
from jax.sharding import PartitionSpec as P

inner_rate = 0.5
outer_rate = 0.7
momentum_coef = 0.9
F32 = jnp.float32
BF16 = jnp.bfloat16


def kernel(
    sizes,
    hid, tgt, w_hbm, outer_hbm, mom_hbm,
    loss_out, grad_out, outer_out, mom_out, next_out,
    w, hbuf, h2d, tbuf, hz, wz, logits, errs, ez, stat, gsend, grecv, outer_v, mom_v, nsend,
    wsem, lsem, hs, hr, ts, tr, zhs, zhr, zws, zwr, hzs, hzr, ss, sr, es, er, gs, gr, ns, nr,
):
    R, T, V, rows, D, vocab, slab, feat, wch, gch = sizes
    n = T * V
    tokens = n * rows
    scale = D ** -0.5
    rep = lax.axis_index("rep")
    g = lax.axis_index("tok") * V + lax.axis_index("voc")

    def group_id(p):
        return {"tok": p // V, "voc": lax.rem(p, V)}

    def over_group(body):
        def step(d, c):
            body(d, lax.rem(g + d, n))
            return c
        lax.fori_loop(1, n, step, 0)

    def over_reps(body):
        for d in range(1, R):
            body(d, lax.rem(rep + d, R))

    def feats(p):
        return pl.ds(pl.multiple_of(p * feat, feat), feat)

    hid_in = pltpu.make_async_copy(hid, hbuf.at[g], lsem.at[0])
    hid_in.start()
    hz_in = pltpu.make_async_copy(hid.at[:, feats(rep)], hz.at[g, rep], lsem.at[1])
    hz_in.start()
    w_in = lambda c: pltpu.make_async_copy(
        w_hbm.at[pl.ds(pl.multiple_of(c * wch, wch), wch)],
        w.at[pl.ds(pl.multiple_of(c * wch, wch), wch)], wsem.at[c])
    for c in range(vocab // wch):
        w_in(c).start()
    outer_in = pltpu.make_async_copy(outer_hbm, outer_v, lsem.at[2])
    outer_in.start()
    mom_in = pltpu.make_async_copy(mom_hbm, mom_v, lsem.at[3])
    mom_in.start()

    diag = lax.broadcasted_iota(jnp.int32, (rows, rows), 0) == lax.broadcasted_iota(jnp.int32, (rows, rows), 1)
    trow = jnp.broadcast_to(tgt[...].astype(F32), (rows, rows))
    tcol = jnp.sum(jnp.where(diag, trow, 0.0), axis=1, keepdims=True)
    tbuf[g] = jnp.broadcast_to(tcol, (rows, 128))

    barrier = pltpu.get_barrier_semaphore()
    over_reps(lambda d, p: pl.semaphore_signal(barrier, inc=1, device_id={"rep": p}))
    over_group(lambda d, p: pl.semaphore_signal(barrier, inc=1, device_id=group_id(p)))
    pl.semaphore_wait(barrier, R - 1 + n - 1)

    def zh(d, p, s):
        return pltpu.make_async_remote_copy(
            hid.at[:, feats(p)], hz.at[g, rep if s else p], zhs.at[d], zhr.at[rep if s else p], device_id={"rep": p})

    def zw(d, p, s):
        return pltpu.make_async_remote_copy(
            w_hbm.at[pl.ds(0, slab), feats(p)], wz.at[rep if s else p], zws.at[d], zwr.at[rep if s else p],
            device_id={"rep": p})

    over_reps(lambda d, p: zh(d, p, True).start())
    hid_in.wait()

    def hx(d, p, s):
        o = g if s else p
        return pltpu.make_async_remote_copy(hbuf.at[g], hbuf.at[o], hs.at[d], hr.at[o], device_id=group_id(p))

    def tx(d, p, s):
        o = g if s else p
        return pltpu.make_async_remote_copy(tbuf.at[g], tbuf.at[o], ts.at[d], tr.at[o], device_id=group_id(p))

    def start_group(d, p):
        hx(d, p, True).start()
        tx(d, p, True).start()
    over_group(start_group)
    over_reps(lambda d, p: zw(d, p, True).start())

    def wait_group(d, p):
        hx(d, p, False).wait_recv()
    over_group(wait_group)

    def pack(i, c):
        cols = pl.ds(pl.multiple_of(i * gch, gch), gch)
        h2d[:, cols] = hbuf[:, :, cols].astype(F32).reshape(tokens, gch).astype(BF16)
        return c
    lax.fori_loop(0, D // gch, pack, 0)

    def logit_step(c, carry):
        w_in(c).wait()
        at = pl.ds(pl.multiple_of(c * wch, wch), wch)
        logits[:, at] = lax.dot_general(
            h2d[...], w[at], (((1,), (1,)), ((), ())), preferred_element_type=F32) * scale
        return carry
    lax.fori_loop(0, vocab // wch, logit_step, 0)

    hz_in.wait()
    over_reps(lambda d, p: zh(d, p, False).wait_recv())

    def hzx(d, p, s):
        o = g if s else p
        return pltpu.make_async_remote_copy(hz.at[g], hz.at[o], hzs.at[d], hzr.at[o], device_id=group_id(p))

    over_group(lambda d, p: tx(d, p, False).wait_recv())
    l = logits[...]
    targets = tbuf[...].reshape(tokens, 128)[:, :1].astype(jnp.int32)
    onehot = targets == g * vocab + lax.broadcasted_iota(jnp.int32, (tokens, vocab), 1)
    top = jnp.max(l, axis=1, keepdims=True)
    ex = jnp.exp(l - top)
    total = jnp.sum(ex, axis=1, keepdims=True)
    tl = jnp.sum(jnp.where(onehot, l, 0.0), axis=1, keepdims=True)
    lanes = stat.shape[2]
    eye = lax.broadcasted_iota(jnp.int32, (tokens, lanes), 0) == lax.broadcasted_iota(jnp.int32, (tokens, lanes), 1)
    to_row = lambda col: jnp.sum(jnp.where(eye, col, 0.0), axis=0, keepdims=True)
    to_col = lambda row: jnp.sum(jnp.where(eye, row, 0.0), axis=1, keepdims=True)
    stat[g] = jnp.concatenate([to_row(top), to_row(total), to_row(tl), jnp.zeros((5, lanes), F32)], axis=0)

    def sx(d, p, s):
        o = g if s else p
        return pltpu.make_async_remote_copy(stat.at[g], stat.at[o], ss.at[d], sr.at[o], device_id=group_id(p))
    over_group(lambda d, p: sx(d, p, True).start())
    over_group(lambda d, p: hzx(d, p, True).start())
    over_group(lambda d, p: sx(d, p, False).wait_recv())
    st = stat[...]
    tops = st[:, 0:1, :]
    all_top = jnp.max(tops, axis=0)
    all_total = jnp.sum(st[:, 1:2, :] * jnp.exp(tops - all_top[None]), axis=0)
    log_total = all_top + jnp.log(all_total)
    loss_row = log_total - jnp.sum(st[:, 2:3, :], axis=0)
    loss_col = to_col(loss_row)
    mine = lax.broadcasted_iota(jnp.int32, (tokens, rows), 0) == g * rows + lax.broadcasted_iota(
        jnp.int32, (tokens, rows), 1)
    loss_out[...] = jnp.sum(jnp.where(mine, loss_col, 0.0), axis=0, keepdims=True)
    err = (jnp.exp(l - to_col(log_total)) - onehot.astype(F32)).astype(BF16)
    errs[...] = err
    ez[rep] = err[:, :slab]

    def zx(d, p, s):
        o = rep if s else p
        return pltpu.make_async_remote_copy(ez.at[rep], ez.at[o], es.at[d], er.at[o], device_id={"rep": p})
    over_reps(lambda d, p: zx(d, p, True).start())

    def grad_step(i, c):
        cols = pl.ds(pl.multiple_of(i * gch, gch), gch)
        part = jnp.dot(errs[...], w[:, cols], preferred_element_type=F32) * scale
        gsend[:, :, cols] = part.reshape(n, rows, gch).astype(BF16)
        return c
    lax.fori_loop(0, D // gch, grad_step, 0)

    def gx(d, p, s):
        return pltpu.make_async_remote_copy(
            gsend.at[p], grecv.at[g if s else p], gs.at[d], gr.at[g if s else p], device_id=group_id(p))
    over_group(lambda d, p: gx(d, p, True).start())

    over_group(lambda d, p: hzx(d, p, False).wait_recv())
    over_reps(lambda d, p: zx(d, p, False).wait_recv())
    outer_in.wait()
    mom_in.wait()
    every_err = ez[...].astype(F32).reshape(R * tokens, slab).T.astype(BF16)
    every_hid = jnp.concatenate(
        [hz[:, r].astype(F32).reshape(tokens, feat).astype(BF16) for r in range(R)], axis=0)
    slab_grad = jnp.dot(every_err, every_hid, preferred_element_type=F32) * scale
    over_reps(lambda d, p: zw(d, p, False).wait_recv())
    wz[rep] = w[:slab, feats(rep)]
    final_sum = jnp.sum(wz[...].astype(F32), axis=0) - inner_rate * slab_grad
    outer = outer_v[...]
    pseudo = outer - final_sum / R
    moved_mom = momentum_coef * mom_v[...] + pseudo
    moved = outer - outer_rate * (pseudo + momentum_coef * moved_mom)
    mom_out[...] = moved_mom
    outer_out[...] = moved
    low = moved.astype(BF16)
    nsend[...] = low

    def nx(d, p, s):
        return pltpu.make_async_remote_copy(
            nsend, next_out.at[:, feats(rep if s else p)], ns.at[d], nr.at[rep if s else p], device_id={"rep": p})
    over_reps(lambda d, p: nx(d, p, True).start())
    next_out[:, feats(rep)] = low

    over_group(lambda d, p: gx(d, p, False).wait_recv())
    grecv[g] = gsend[g]

    def grad_sum(i, c):
        cols = pl.ds(pl.multiple_of(i * gch, gch), gch)
        grad_out[:, cols] = jnp.sum(grecv[:, :, cols].astype(F32), axis=0)
        return c
    lax.fori_loop(0, D // gch, grad_sum, 0)

    def drain_group(d, p):
        for x in (hx, tx, hzx, sx, gx):
            x(d, p, True).wait_send()
    over_group(drain_group)

    def drain_reps(d, p):
        for x in (zh, zw, zx, nx):
            x(d, p, True).wait_send()
    over_reps(drain_reps)
    over_reps(lambda d, p: nx(d, p, False).wait_recv())


def per_device(hidden, targets, unembed, outer_weight, momentum):
    R, T, V = lax.axis_size("rep"), lax.axis_size("tok"), lax.axis_size("voc")
    n = T * V
    _, rows, D = hidden.shape
    vocab = unembed.shape[1]
    slab, feat = outer_weight.shape
    tokens = n * rows
    lanes = -(-tokens // 128) * 128
    wch = min(256, vocab)
    gch = min(512, D)
    dma = pltpu.SemaphoreType.DMA
    vm = pltpu.VMEM
    spec_v = pl.BlockSpec(memory_space=pltpu.VMEM)
    spec_a = pl.BlockSpec(memory_space=pl.ANY)
    scratch = [
        vm((vocab, D), BF16), vm((n, rows, D), BF16), vm((tokens, D), BF16), vm((n, rows, 128), F32),
        vm((n, R, rows, feat), BF16), vm((R, slab, feat), BF16), vm((tokens, vocab), F32),
        vm((tokens, vocab), BF16), vm((R, tokens, slab), BF16), vm((n, 8, lanes), F32),
        vm((n, rows, D), BF16), vm((n, rows, D), BF16), vm((slab, feat), F32), vm((slab, feat), F32),
        vm((slab, feat), BF16),
        dma((vocab // wch,)), dma((4,)),
        dma((n,)), dma((n,)), dma((n,)), dma((n,)), dma((R,)), dma((R,)), dma((R,)), dma((R,)),
        dma((n,)), dma((n,)), dma((n,)), dma((n,)), dma((R,)), dma((R,)), dma((n,)), dma((n,)), dma((R,)), dma((R,)),
    ]
    loss, grad, new_outer, new_mom, nxt = pl.pallas_call(
        functools.partial(kernel, (R, T, V, rows, D, vocab, slab, feat, wch, gch)),
        out_shape=(
            jax.ShapeDtypeStruct((1, rows), F32),
            jax.ShapeDtypeStruct((rows, D), F32),
            jax.ShapeDtypeStruct((slab, feat), F32),
            jax.ShapeDtypeStruct((slab, feat), F32),
            jax.ShapeDtypeStruct((slab, R * feat), BF16),
        ),
        in_specs=[spec_a, spec_v, spec_a, spec_a, spec_a],
        out_specs=(spec_v,) * 5,
        scratch_shapes=scratch,
        compiler_params=pltpu.CompilerParams(
            collective_id=0, has_side_effects=True, vmem_limit_bytes=60 * 1024 * 1024),
        name="step",
    )(hidden[0], targets, unembed[0], outer_weight, momentum)
    return (loss, grad[None], new_outer, new_mom, nxt)


def solution(mesh):
    group = ("tok", "voc")
    return jax.shard_map(
        per_device,
        mesh=mesh,
        in_specs=(P("rep", group, None), P("rep", group), P("rep", group, None), P(group, "rep"), P(group, "rep")),
        out_specs=(P("rep", group), P("rep", group, None), P(group, "rep"), P(group, "rep"), P(group, None)),
        check_vma=False,
    )
```

time: 171 us -> 67.6 us (0.40)
  the two profiles are of different devices: /device:TPU:0 before, /device:TPU:24 now
where the time goes in v1:
time: 67.6 us; the launch traced here: 67.3 us
  Pallas kernels  57.9 us (86%)
  local copies, waits for them, and re-layouts  8.8 us (13%)
    pallas_call x1, Pallas kernels, per_device(): pl.pallas_call(functools.partial(kernel, (R, T, V, rows, D, vocab, slab,...  57.9 us
    unnamed x5, local copies, waits for them, and re-layouts  8.8 us

profile of v1, /device:TPU:24, one launch (start us, length us, event | category | flops | bytes accessed | tf_op | source)
XLA Modules:
  0.0 67.3 jit_solution(9732879756301889836)
XLA Ops:
  0.6 57.9 %step.1 = (f32[1,8]{1,0:T(1,128)}, f32[8,4096]{1,0:T(8,128)}, f32[128,1024]{1,0:T(8,128)}, f32[128,1024]{1,0:T(8,128)}, bf16[128,4096]{1,0:T(8,128)(2,1)}) custom-call(bf16[8,4096]{1,0:T(8,128)(2,1)} %bitcast.5, s32[1,8]{1,0:T(1,128)} %tgt.1, bf16[1024,4096]{1,0:T(8,128)(2,1)} %bitcast.3, f32[128,1024]{1,0:T(8,128)} %outer_hbm.1, f32[128,1024]{1,0:T(8,128)} %mom_hbm.1), custom_call_target="tpu_custom_call" | custom-call | tf_op jit(solution)/shard_map/step/pallas_call | solution.py:244
  58.5 1.2 %copy.15 = f32[1,8]{1,0:T(1,128)} copy(f32[1,8]{1,0:T(1,128)} %get-tuple-element.20) | data formatting | bytes 64
  59.7 1.6 %copy.16 = f32[1,8,4096]{2,1,0:T(8,128)} copy(f32[1,8,4096]{2,1,0:T(8,128)} %bitcast.4) | data formatting | bytes 262144
  61.2 1.9 %copy.17 = f32[128,1024]{1,0:T(8,128)} copy(f32[128,1024]{1,0:T(8,128)} %get-tuple-element.22) | data formatting | bytes 1048576
  63.1 1.9 %copy.18 = f32[128,1024]{1,0:T(8,128)} copy(f32[128,1024]{1,0:T(8,128)} %get-tuple-element.23) | data formatting | bytes 1048576
  65.0 2.3 %copy.19 = bf16[128,4096]{1,0:T(8,128)(2,1)} copy(bf16[128,4096]{1,0:T(8,128)(2,1)} %get-tuple-element.24) | data formatting | bytes 2097152

commit v2 on v1

--- a/solution.py
+++ b/solution.py
@@ -16,12 +16,13 @@
 
 def kernel(
     sizes,
-    hid, tgt, w_hbm, outer_hbm, mom_hbm,
+    hid, tgt, w_hbm, outer_v, mom_v,
     loss_out, grad_out, outer_out, mom_out, next_out,
-    w, hbuf, h2d, tbuf, hz, wz, logits, errs, ez, stat, gsend, grecv, outer_v, mom_v, nsend,
-    wsem, lsem, hs, hr, ts, tr, zhs, zhr, zws, zwr, hzs, hzr, ss, sr, es, er, gs, gr, ns, nr,
+    w, hbuf, h2d, tbuf, hz, wz, logits, errs, ez, stat, gsend, grecv, sgrad,
+    wsem, lsem, hs, hr, ts, tr, zhs, zhr, zws, zwr, hzs, hzr, ss, sr, es, er, gs, gr, nright, nleft, nr,
 ):
-    R, T, V, rows, D, vocab, slab, feat, wch, gch = sizes
+    R, T, V, rows, D, vocab, slab, feat, wch, gch, parts = sizes
+    prow = slab // parts
     n = T * V
     tokens = n * rows
     scale = D ** -0.5
@@ -53,10 +54,6 @@
         w.at[pl.ds(pl.multiple_of(c * wch, wch), wch)], wsem.at[c])
     for c in range(vocab // wch):
         w_in(c).start()
-    outer_in = pltpu.make_async_copy(outer_hbm, outer_v, lsem.at[2])
-    outer_in.start()
-    mom_in = pltpu.make_async_copy(mom_hbm, mom_v, lsem.at[3])
-    mom_in.start()
 
     diag = lax.broadcasted_iota(jnp.int32, (rows, rows), 0) == lax.broadcasted_iota(jnp.int32, (rows, rows), 1)
     trow = jnp.broadcast_to(tgt[...].astype(F32), (rows, rows))
@@ -72,9 +69,10 @@
         return pltpu.make_async_remote_copy(
             hid.at[:, feats(p)], hz.at[g, rep if s else p], zhs.at[d], zhr.at[rep if s else p], device_id={"rep": p})
 
-    def zw(d, p, s):
+    def zw(k, d, p, s):
+        o = rep if s else p
         return pltpu.make_async_remote_copy(
-            w_hbm.at[pl.ds(0, slab), feats(p)], wz.at[rep if s else p], zws.at[d], zwr.at[rep if s else p],
+            w_hbm.at[pl.ds(k * prow, prow), feats(p)], wz.at[o, pl.ds(k * prow, prow)], zws.at[k, d], zwr.at[k, o],
             device_id={"rep": p})
 
     over_reps(lambda d, p: zh(d, p, True).start())
@@ -92,7 +90,8 @@
         hx(d, p, True).start()
         tx(d, p, True).start()
     over_group(start_group)
-    over_reps(lambda d, p: zw(d, p, True).start())
+    for k in range(parts):
+        over_reps(lambda d, p: zw(k, d, p, True).start())
 
     def wait_group(d, p):
         hx(d, p, False).wait_recv()
@@ -172,29 +171,51 @@
 
     over_group(lambda d, p: hzx(d, p, False).wait_recv())
     over_reps(lambda d, p: zx(d, p, False).wait_recv())
-    outer_in.wait()
-    mom_in.wait()
     every_err = ez[...].astype(F32).reshape(R * tokens, slab).T.astype(BF16)
     every_hid = jnp.concatenate(
         [hz[:, r].astype(F32).reshape(tokens, feat).astype(BF16) for r in range(R)], axis=0)
-    slab_grad = jnp.dot(every_err, every_hid, preferred_element_type=F32) * scale
-    over_reps(lambda d, p: zw(d, p, False).wait_recv())
+    sgrad[...] = jnp.dot(every_err, every_hid, preferred_element_type=F32) * scale
     wz[rep] = w[:slab, feats(rep)]
-    final_sum = jnp.sum(wz[...].astype(F32), axis=0) - inner_rate * slab_grad
-    outer = outer_v[...]
-    pseudo = outer - final_sum / R
-    moved_mom = momentum_coef * mom_v[...] + pseudo
-    moved = outer - outer_rate * (pseudo + momentum_coef * moved_mom)
-    mom_out[...] = moved_mom
-    outer_out[...] = moved
-    low = moved.astype(BF16)
-    nsend[...] = low
-
-    def nx(d, p, s):
+
+    def nx(k, b, side):
+        at = next_out.at[pl.ds(k * prow, prow), feats(b)]
+        sems = nright if side > 0 else nleft
         return pltpu.make_async_remote_copy(
-            nsend, next_out.at[:, feats(rep if s else p)], ns.at[d], nr.at[rep if s else p], device_id={"rep": p})
-    over_reps(lambda d, p: nx(d, p, True).start())
-    next_out[:, feats(rep)] = low
+            at, at, sems.at[k, b], nr.at[k, b], device_id={"rep": lax.rem(rep + side + R, R)})
+
+    has_right, has_left = rep < R - 1, rep > 0
+
+    def outer_part(k):
+        at = pl.ds(k * prow, prow)
+        over_reps(lambda d, p: zw(k, d, p, False).wait_recv())
+        final_sum = jnp.sum(wz[:, at].astype(F32), axis=0) - inner_rate * sgrad[at]
+        outer = outer_v[at]
+        pseudo = outer - final_sum / R
+        moved_mom = momentum_coef * mom_v[at] + pseudo
+        moved = outer - outer_rate * (pseudo + momentum_coef * moved_mom)
+        mom_out[at] = moved_mom
+        outer_out[at] = moved
+        next_out[at, feats(rep)] = moved.astype(BF16)
+        pl.when(has_right)(lambda: nx(k, rep, 1).start())
+        pl.when(has_left)(lambda: nx(k, rep, -1).start())
+
+    def relay(k):
+        for d in range(1, R):
+            @pl.when(rep >= d)
+            def _():
+                nx(k, rep - d, 1).wait_recv()
+                pl.when(has_right)(lambda: nx(k, rep - d, 1).start())
+
+            @pl.when(rep + d < R)
+            def _():
+                nx(k, rep + d, -1).wait_recv()
+                pl.when(has_left)(lambda: nx(k, rep + d, -1).start())
+
+    for k in range(parts):
+        outer_part(k)
+        if k > 0:
+            relay(k - 1)
+    relay(parts - 1)
 
     over_group(lambda d, p: gx(d, p, False).wait_recv())
     grecv[g] = gsend[g]
@@ -211,10 +232,25 @@
     over_group(drain_group)
 
     def drain_reps(d, p):
-        for x in (zh, zw, zx, nx):
+        for x in (zh, zx):
             x(d, p, True).wait_send()
+        for k in range(parts):
+            zw(k, d, p, True).wait_send()
     over_reps(drain_reps)
-    over_reps(lambda d, p: nx(d, p, False).wait_recv())
+    for k in range(parts):
+        for d in range(R):
+            pl.when(jnp.logical_and(has_right, rep >= d))(lambda: nx(k, rep - d, 1).wait_send())
+            pl.when(jnp.logical_and(has_left, rep + d < R))(lambda: nx(k, rep + d, -1).wait_send())
+
+
+def flush(*refs):
+    count = len(refs) // 2
+    sems = refs[-1]
+    copies = [pltpu.make_async_copy(refs[i], refs[count + i], sems.at[i]) for i in range(count)]
+    for c in copies:
+        c.start()
+    for c in copies:
+        c.wait()
 
 
 def per_device(hidden, targets, unembed, outer_weight, momentum):
@@ -227,22 +263,24 @@
     lanes = -(-tokens // 128) * 128
     wch = min(256, vocab)
     gch = min(512, D)
+    parts = 4 if slab % 128 == 0 else 1
     dma = pltpu.SemaphoreType.DMA
     vm = pltpu.VMEM
     spec_v = pl.BlockSpec(memory_space=pltpu.VMEM)
-    spec_a = pl.BlockSpec(memory_space=pl.ANY)
+    spec_a = pl.BlockSpec(memory_space=pltpu.HBM)
     scratch = [
         vm((vocab, D), BF16), vm((n, rows, D), BF16), vm((tokens, D), BF16), vm((n, rows, 128), F32),
         vm((n, R, rows, feat), BF16), vm((R, slab, feat), BF16), vm((tokens, vocab), F32),
         vm((tokens, vocab), BF16), vm((R, tokens, slab), BF16), vm((n, 8, lanes), F32),
-        vm((n, rows, D), BF16), vm((n, rows, D), BF16), vm((slab, feat), F32), vm((slab, feat), F32),
-        vm((slab, feat), BF16),
-        dma((vocab // wch,)), dma((4,)),
-        dma((n,)), dma((n,)), dma((n,)), dma((n,)), dma((R,)), dma((R,)), dma((R,)), dma((R,)),
-        dma((n,)), dma((n,)), dma((n,)), dma((n,)), dma((R,)), dma((R,)), dma((n,)), dma((n,)), dma((R,)), dma((R,)),
+        vm((n, rows, D), BF16), vm((n, rows, D), BF16),
+        vm((slab, feat), F32),
+        dma((vocab // wch,)), dma((2,)),
+        dma((n,)), dma((n,)), dma((n,)), dma((n,)), dma((R,)), dma((R,)), dma((parts, R)), dma((parts, R)),
+        dma((n,)), dma((n,)), dma((n,)), dma((n,)), dma((R,)), dma((R,)), dma((n,)), dma((n,)),
+        dma((parts, R)), dma((parts, R)), dma((parts, R)),
     ]
-    loss, grad, new_outer, new_mom, nxt = pl.pallas_call(
-        functools.partial(kernel, (R, T, V, rows, D, vocab, slab, feat, wch, gch)),
+    results = pl.pallas_call(
+        functools.partial(kernel, (R, T, V, rows, D, vocab, slab, feat, wch, gch, parts)),
         out_shape=(
             jax.ShapeDtypeStruct((1, rows), F32),
             jax.ShapeDtypeStruct((rows, D), F32),
@@ -250,13 +288,22 @@
             jax.ShapeDtypeStruct((slab, feat), F32),
             jax.ShapeDtypeStruct((slab, R * feat), BF16),
         ),
-        in_specs=[spec_a, spec_v, spec_a, spec_a, spec_a],
+        in_specs=[spec_a, spec_v, spec_a, spec_v, spec_v],
         out_specs=(spec_v,) * 5,
         scratch_shapes=scratch,
         compiler_params=pltpu.CompilerParams(
-            collective_id=0, has_side_effects=True, vmem_limit_bytes=60 * 1024 * 1024),
+            collective_id=0, has_side_effects=True, vmem_limit_bytes=50 * 2**20),
         name="step",
     )(hidden[0], targets, unembed[0], outer_weight, momentum)
+    loss, grad, new_outer, new_mom, nxt = pl.pallas_call(
+        flush,
+        out_shape=tuple(jax.ShapeDtypeStruct(x.shape, x.dtype) for x in results),
+        in_specs=[spec_v] * 5,
+        out_specs=(spec_a,) * 5,
+        scratch_shapes=[dma((5,))],
+        compiler_params=pltpu.CompilerParams(vmem_limit_bytes=6 * 2**20),
+        name="flush",
+    )(*results)
     return (loss, grad[None], new_outer, new_mom, nxt)
 
 

time: 67.6 us -> 65.8 us (0.973)
  the two profiles are of different devices: /device:TPU:24 before, /device:TPU:0 now
where the time goes in v2:
time: 65.8 us; the launch traced here: 65.6 us
  Pallas kernels  61.3 us (93%)
  local copies, waits for them, and re-layouts  3.57 us (5%)
    pallas_call x1, Pallas kernels, per_device(): pl.pallas_call(functools.partial(kernel, (R, T, V, rows, D, vocab, slab,...  59.9 us
    unnamed x8, local copies, waits for them, and re-layouts  3.57 us
    pallas_call x1, Pallas kernels, per_device(): pl.pallas_call(flush, out_shape=tuple((jax.ShapeDtypeStruct(x.shape, x.dt...  1.41 us

profile of v2, /device:TPU:0, one launch (start us, length us, event | category | flops | bytes accessed | tf_op | source)
XLA Modules:
  0.0 65.6 jit_solution(18231790173436219678)
XLA Ops:
  0.6 0.0 copy-start
  0.6 1.0 %copy-done = f32[128,1024]{1,0:T(8,128)S(1)} copy-done((f32[128,1024]{1,0:T(8,128)S(1)}, f32[128,1024]{1,0:T(8,128)}, u32[]{:S(2)}) %copy-start) | copy-done | bytes 524312
  1.7 0.0 copy-start.1
  1.7 1.0 %copy-done.1 = f32[128,1024]{1,0:T(8,128)S(1)} copy-done((f32[128,1024]{1,0:T(8,128)S(1)}, f32[128,1024]{1,0:T(8,128)}, u32[]{:S(2)}) %copy-start.1) | copy-done | bytes 524312
  2.7 0.0 copy-start.2
  2.7 0.8 %copy-done.2 = bf16[1,8,4096]{2,1,0:T(8,128)(2,1)S(1)} copy-done((bf16[1,8,4096]{2,1,0:T(8,128)(2,1)S(1)}, bf16[1,8,4096]{2,1,0:T(8,128)(2,1)}, u32[]{:S(2)}) %copy-start.2) | copy-done | bytes 65560
  3.6 0.0 copy-start.3
  3.6 0.7 copy-done.3
  4.2 59.9 %step.1 = (f32[1,8]{1,0:T(1,128)S(1)}, f32[8,4096]{1,0:T(8,128)S(1)}, f32[128,1024]{1,0:T(8,128)S(1)}, f32[128,1024]{1,0:T(8,128)S(1)}, bf16[128,4096]{1,0:T(8,128)(2,1)S(1)}) custom-call(bf16[8,4096]{1,0:T(8,128)(2,1)S(1)} %bitcast.3, s32[1,8]{1,0:T(1,128)S(1)} %copy-done.3, bf16[1024,4096]{1,0:T(8,128)(2,1)} %bitcast.4, f32[128,1024]{1,0:T(8,128)S(1)} %copy-done, ...), custom_call_target="tpu_custom_call" | custom-call | tf_op jit(solution)/shard_map/step/pallas_call | solution.py:282
  64.2 1.4 %flush.1 = (f32[1,8]{1,0:T(1,128)}, f32[8,4096]{1,0:T(8,128)}, f32[128,1024]{1,0:T(8,128)}, f32[128,1024]{1,0:T(8,128)}, bf16[128,4096]{1,0:T(8,128)(2,1)}) custom-call(f32[1,8]{1,0:T(1,128)S(1)} %get-tuple-element.15.refs_0_, f32[8,4096]{1,0:T(8,128)S(1)} %get-tuple-element.16.refs_1_, f32[128,1024]{1,0:T(8,128)S(1)} %get-tuple-element.17.refs_2_, ...), custom_call_target="tpu_custom_call" | custom-call | tf_op jit(solution)/shard_map/flush/pallas_call | solution.py:298
Async XLA Ops:
  0.6 1.0 %copy-start = (f32[128,1024]{1,0:T(8,128)S(1)}, f32[128,1024]{1,0:T(8,128)}, u32[]{:S(2)}) copy-start(f32[128,1024]{1,0:T(8,128)} %outer_v.1) | copy-start | bytes 1572868
  1.7 1.0 %copy-start.1 = (f32[128,1024]{1,0:T(8,128)S(1)}, f32[128,1024]{1,0:T(8,128)}, u32[]{:S(2)}) copy-start(f32[128,1024]{1,0:T(8,128)} %mom_v.1) | copy-start | bytes 1572868
  2.7 0.8 %copy-start.2 = (bf16[1,8,4096]{2,1,0:T(8,128)(2,1)S(1)}, bf16[1,8,4096]{2,1,0:T(8,128)(2,1)}, u32[]{:S(2)}) copy-start(bf16[1,8,4096]{2,1,0:T(8,128)(2,1)} %param.5) | copy-start | bytes 196612
  3.6 0.7 copy-start.3

commit v3 on v2

--- a/solution.py
+++ b/solution.py
@@ -90,7 +90,7 @@
         hx(d, p, True).start()
         tx(d, p, True).start()
     over_group(start_group)
-    for k in range(parts):
+    for k in range(max(parts - 1, 1)):
         over_reps(lambda d, p: zw(k, d, p, True).start())
 
     def wait_group(d, p):
@@ -156,18 +156,18 @@
         o = rep if s else p
         return pltpu.make_async_remote_copy(ez.at[rep], ez.at[o], es.at[d], er.at[o], device_id={"rep": p})
     over_reps(lambda d, p: zx(d, p, True).start())
+    for k in range(1, parts)[-1:]:
+        over_reps(lambda d, p: zw(k, d, p, True).start())
 
     def grad_step(i, c):
         cols = pl.ds(pl.multiple_of(i * gch, gch), gch)
         part = jnp.dot(errs[...], w[:, cols], preferred_element_type=F32) * scale
         gsend[:, :, cols] = part.reshape(n, rows, gch).astype(BF16)
         return c
-    lax.fori_loop(0, D // gch, grad_step, 0)
 
     def gx(d, p, s):
         return pltpu.make_async_remote_copy(
             gsend.at[p], grecv.at[g if s else p], gs.at[d], gr.at[g if s else p], device_id=group_id(p))
-    over_group(lambda d, p: gx(d, p, True).start())
 
     over_group(lambda d, p: hzx(d, p, False).wait_recv())
     over_reps(lambda d, p: zx(d, p, False).wait_recv())
@@ -211,11 +211,14 @@
                 nx(k, rep + d, -1).wait_recv()
                 pl.when(has_left)(lambda: nx(k, rep + d, -1).start())
 
+    for k in range(max(parts - 1, 1)):
+        outer_part(k)
+    lax.fori_loop(0, D // gch, grad_step, 0)
+    over_group(lambda d, p: gx(d, p, True).start())
+    for k in range(1, parts)[-1:]:
+        outer_part(k)
     for k in range(parts):
-        outer_part(k)
-        if k > 0:
-            relay(k - 1)
-    relay(parts - 1)
+        relay(k)
 
     over_group(lambda d, p: gx(d, p, False).wait_recv())
     grecv[g] = gsend[g]

time: 65.8 us -> 59.8 us (0.909)
  Pallas kernels: 61.3 us -> 55.3 us
    pallas_call x1, Pallas kernels: 59.9 us -> 53.9 us  [per_device(): pl.pallas_call(functools.partial(kernel, (R, T, V, rows, D, vocab, slab,...]
where the time goes in v3:
time: 59.8 us; the launch traced here: 59.5 us
  Pallas kernels  55.3 us (92%)
  local copies, waits for them, and re-layouts  3.57 us (6%)
  between operations  0.65 us (1%)
    pallas_call x1, Pallas kernels, per_device(): pl.pallas_call(functools.partial(kernel, (R, T, V, rows, D, vocab, slab,...  53.9 us
    unnamed x8, local copies, waits for them, and re-layouts  3.57 us
    pallas_call x1, Pallas kernels, per_device(): pl.pallas_call(flush, out_shape=tuple((jax.ShapeDtypeStruct(x.shape, x.dt...  1.41 us

profile of v3, /device:TPU:0, one launch (start us, length us, event | category | flops | bytes accessed | tf_op | source)
XLA Modules:
  0.0 59.5 jit_solution(1394376001163861443)
XLA Ops:
  0.6 0.0 copy-start
  0.6 1.0 %copy-done = f32[128,1024]{1,0:T(8,128)S(1)} copy-done((f32[128,1024]{1,0:T(8,128)S(1)}, f32[128,1024]{1,0:T(8,128)}, u32[]{:S(2)}) %copy-start) | copy-done | bytes 524312
  1.7 0.0 copy-start.1
  1.7 1.0 %copy-done.1 = f32[128,1024]{1,0:T(8,128)S(1)} copy-done((f32[128,1024]{1,0:T(8,128)S(1)}, f32[128,1024]{1,0:T(8,128)}, u32[]{:S(2)}) %copy-start.1) | copy-done | bytes 524312
  2.7 0.0 copy-start.2
  2.7 0.8 %copy-done.2 = bf16[1,8,4096]{2,1,0:T(8,128)(2,1)S(1)} copy-done((bf16[1,8,4096]{2,1,0:T(8,128)(2,1)S(1)}, bf16[1,8,4096]{2,1,0:T(8,128)(2,1)}, u32[]{:S(2)}) %copy-start.2) | copy-done | bytes 65560
  3.6 0.0 copy-start.3
  3.6 0.7 %copy-done.3 = s32[1,8]{1,0:T(1,128)S(1)} copy-done((s32[1,8]{1,0:T(1,128)S(1)}, s32[1,8]{1,0:T(1,128)}, u32[]{:S(2)}) %copy-start.3) | copy-done | bytes 56
  4.2 53.9 %step.1 = (f32[1,8]{1,0:T(1,128)S(1)}, f32[8,4096]{1,0:T(8,128)S(1)}, f32[128,1024]{1,0:T(8,128)S(1)}, f32[128,1024]{1,0:T(8,128)S(1)}, bf16[128,4096]{1,0:T(8,128)(2,1)S(1)}) custom-call(bf16[8,4096]{1,0:T(8,128)(2,1)S(1)} %bitcast.3, s32[1,8]{1,0:T(1,128)S(1)} %copy-done.3, bf16[1024,4096]{1,0:T(8,128)(2,1)} %bitcast.4, f32[128,1024]{1,0:T(8,128)S(1)} %copy-done, ...), custom_call_target="tpu_custom_call" | custom-call | tf_op jit(solution)/shard_map/step/pallas_call | solution.py:285
  58.1 1.4 %flush.1 = (f32[1,8]{1,0:T(1,128)}, f32[8,4096]{1,0:T(8,128)}, f32[128,1024]{1,0:T(8,128)}, f32[128,1024]{1,0:T(8,128)}, bf16[128,4096]{1,0:T(8,128)(2,1)}) custom-call(f32[1,8]{1,0:T(1,128)S(1)} %get-tuple-element.15.refs_0_, f32[8,4096]{1,0:T(8,128)S(1)} %get-tuple-element.16.refs_1_, f32[128,1024]{1,0:T(8,128)S(1)} %get-tuple-element.17.refs_2_, ...), custom_call_target="tpu_custom_call" | custom-call | tf_op jit(solution)/shard_map/flush/pallas_call | solution.py:301
Async XLA Ops:
  0.6 1.0 %copy-start = (f32[128,1024]{1,0:T(8,128)S(1)}, f32[128,1024]{1,0:T(8,128)}, u32[]{:S(2)}) copy-start(f32[128,1024]{1,0:T(8,128)} %outer_v.1) | copy-start | bytes 1572868
  1.7 1.0 %copy-start.1 = (f32[128,1024]{1,0:T(8,128)S(1)}, f32[128,1024]{1,0:T(8,128)}, u32[]{:S(2)}) copy-start(f32[128,1024]{1,0:T(8,128)} %mom_v.1) | copy-start | bytes 1572868
  2.7 0.8 %copy-start.2 = (bf16[1,8,4096]{2,1,0:T(8,128)(2,1)S(1)}, bf16[1,8,4096]{2,1,0:T(8,128)(2,1)}, u32[]{:S(2)}) copy-start(bf16[1,8,4096]{2,1,0:T(8,128)(2,1)} %param.5) | copy-start | bytes 196612
  3.6 0.7 %copy-start.3 = (s32[1,8]{1,0:T(1,128)S(1)}, s32[1,8]{1,0:T(1,128)}, u32[]{:S(2)}) copy-start(s32[1,8]{1,0:T(1,128)} %tgt.1) | copy-start | bytes 100
